TPU v7x, 256 devices: a whole 4x4x8 slice. The times are simulated.
256 devices in a mesh: dp: 16 (over z, core), mp: 16 (over y, x).
Axes of the slice: x: 4, y: 4, z: 8, core: 2. Of those that a mesh axis runs over, the one named last changes fastest.
Arguments:
- inputs: bfloat16 [4096, 8192], P('dp', 'mp'), may hold values from -6 to 6
- out_grads: bfloat16 [4096, 8192], P('dp', 'mp'), may hold values from -6 to 6
- left_old: float32 [8192, 8192], P('dp', 'mp'), may hold values from -2 to 4, as said below
- right_old: float32 [8192, 8192], P('dp', 'mp'), may hold values from -2 to 4, as said below
- left_roots: float32 [8192, 8192], P('dp', 'mp'), may hold values from -2 to 4, as said below
- right_roots: float32 [8192, 8192], P('dp', 'mp'), may hold values from -2 to 4, as said below
- ages: int32 [16, 16], replicated, may hold values from 0 to 199, as said below
Outputs:
- precond: float32 [8192, 8192], P('dp', 'mp')
- left_new: float32 [8192, 8192], P('dp', 'mp')
- right_new: float32 [8192, 8192], P('dp', 'mp')
Inputs may be any that keep to these rules, and one draw needn't show every extreme that they name: `ages`: in every row i, blocks (i, j) and (i, j + 8) are never both due, and every row has a due block. `left_old`: every 512 x 512 block is symmetric and positive definite. `right_old`: every 512 x 512 block is symmetric and positive definite. `left_roots`: every 512 x 512 block is symmetric and positive definite. `right_roots`: every 512 x 512 block is symmetric and positive definite.
All inputs are finite; a program needn't handle non-finite values.
Results may differ from a plain program's by a relative error of at most 0.001.
Values may be sent and summed in bfloat16 or wider, within the bound.
A program may use at most 128 MiB of HBM per device.

v0:
```python
import jax
import jax.numpy as jnp
from jax import lax
from jax.experimental import pallas as pl
from jax.experimental.pallas import tpu as pltpu
from jax.sharding import PartitionSpec as P

ITERS = 3
PERIOD = 100
NZ, NY, NX = 8, 4, 4
PARTS = 16
MESH = pl.DeviceIdType.MESH

decay_rate = 0.95
ridge = 0.001


UNITS = 4
SHIFT = (0, 6, 8, 14)
ORDER = (
    ("enter", 0), ("enter", 1), ("enter", 2), ("enter", 3), ("own", 0), ("own", 1), ("forward", 0),
    ("forward", 1), ("forward", 2), ("forward", 3), ("ring", 1, 0, -1), ("first", 0), ("first", 1),
    ("first", 2), ("first", 3), ("side", 0, 0, 1), ("ring", 1, 0, 1), ("near", 0, 1), ("near", 0, -1),
    ("own", 2), ("own", 3), ("near", 1, -1), ("near", 3, -1), ("ring", 1, 2, 1), ("side", 0, 0, -1),
    ("side", 2, 0, -1), ("ring", 1, 3, -1), ("ring", 1, 1, -1), ("side", 1, 0, -1), ("ring", 1, 3, 1),
    ("near", 2, 1), ("near", 2, -1), ("ring", 1, 1, 1), ("near", 1, 1), ("near", 3, 1),
    ("side", 2, 0, 1), ("side", 3, 0, -1), ("ring", 1, 2, -1), ("ring", 2, 0, 1), ("ring", 2, 0, -1),
    ("far", 0), ("side", 2, -1, -1), ("side", 1, 0, 1), ("ring", 2, 1, 1), ("far", 3), ("far", 2),
    ("ring", 2, 2, 1), ("far", 1), ("side", 0, -1, 1), ("ring", 2, 3, 1), ("ring", 2, 1, -1),
    ("side", 3, -1, 1), ("ring", 2, 3, -1), ("side", 0, 1, -1), ("side", 3, 1, 1), ("side", 3, 0, 1),
    ("side", 3, 1, -1), ("side", 0, 2, -1), ("ring", 2, 2, -1), ("side", 1, -1, -1), ("side", 1, 1, 1),
    ("side", 1, -1, 1), ("side", 3, -1, -1), ("side", 0, -1, -1), ("side", 0, 1, 1), ("ring", 3, 1, 1),
    ("ring", 3, 0, 1), ("side", 2, 1, 1), ("side", 1, 2, 1), ("side", 1, 1, -1), ("side", 2, -1, 1),
    ("ring", 3, 1, -1), ("side", 2, 2, -1), ("side", 0, 2, 1), ("side", 1, 2, -1), ("side", 2, 1, -1),
    ("ring", 3, 3, -1), ("ring", 3, 2, -1), ("side", 2, 2, 1), ("ring", 3, 3, 1), ("side", 3, 2, 1),
    ("ring", 3, 0, -1), ("side", 3, 2, -1), ("ring", 3, 2, 1), ("last", 1), ("last", 2), ("last", 3),
    ("last", 0),
)


def gather_kernel(
    scale, a_hbm, b_hbm, g_ref, abuf, bbuf, stage, load_sem, s_send, s_recv, t_send, t_recv,
    a_send, a_recv, b_send, b_recv,
):
    rows, width = a_hbm.shape
    count = rows // UNITS
    i = lax.axis_index("dp")
    k = lax.axis_index("mp")
    z, c = i // 2, i % 2
    y, x = k // NX, k % NX

    def place(dz=0, dy=0, dx=0, other=False):
        core = 1 - c if other else c
        return {
            "dp": ((z + dz + NZ) % NZ) * 2 + core,
            "mp": ((y + dy + NY) % NY) * NX + (x + dx + NX) % NX,
        }

    def near(u):
        return {"dp": i, "mp": (i + k + SHIFT[u]) % PARTS}

    def near_origin(u):
        return {"dp": i, "mp": (k - i - SHIFT[u] + 2 * PARTS) % PARTS}

    def token_block(u):
        return (k - i - SHIFT[u] + 2 * PARTS) % PARTS

    def partner(u):
        return {"dp": token_block(u), "mp": k}

    def stays(u):
        return (i + SHIFT[u]) % PARTS == 0

    def rows_of(u):
        return pl.ds(u * count, count)

    load = pltpu.make_async_copy(b_hbm, bbuf.at[i], load_sem.at[0])
    load.start()
    barrier = pltpu.get_barrier_semaphore()
    greeted = [
        place(dz=1), place(dz=-1), place(dy=1), place(dy=-1), place(dx=1), place(dx=-1),
        place(other=True),
    ]
    greeted += [device(u) for u in range(UNITS) for device in (near_origin, partner)]
    for device in greeted:
        pl.semaphore_signal(barrier, inc=1, device_id=device, device_id_type=MESH)
    pl.semaphore_wait(barrier, len(greeted))

    def first_hop(u, final, local):
        source = a_hbm.at[rows_of(u)]
        goal = abuf.at[i, rows_of(u)] if final else stage.at[u]
        arrived = (t_recv if final else s_recv).at[u]
        if local:
            return pltpu.make_async_copy(source, goal, arrived)
        return pltpu.make_async_remote_copy(
            src_ref=source,
            dst_ref=goal,
            send_sem=s_send.at[u],
            recv_sem=arrived,
            device_id=near(u),
            device_id_type=MESH,
        )

    def second_hop(u, slot):
        return pltpu.make_async_remote_copy(
            src_ref=stage.at[u],
            dst_ref=abuf.at[slot, rows_of(u)],
            send_sem=t_send.at[u],
            recv_sem=t_recv.at[u],
            device_id=partner(u),
            device_id_type=MESH,
        )

    def start_first_hop(u):
        for final in (False, True):
            for local in (False, True):

                @pl.when(((i == k) == final) & (stays(u) == local))
                def _():
                    first_hop(u, final, local).start()

    def forward(u):
        for local in (False, True):

            @pl.when((token_block(u) != i) & (stays(u) == local))
            def _():
                copy = first_hop(u, False, local)
                if local:
                    copy.wait()
                else:
                    copy.wait_recv()

        @pl.when(token_block(u) != i)
        def _():
            second_hop(u, i).start()

    def entered(u):
        @pl.when(token_block(u) != i)
        def _():
            second_hop(u, token_block(u)).wait_recv()

        for local in (False, True):

            @pl.when((token_block(u) == i) & (stays(u) == local))
            def _():
                copy = first_hop(u, True, local)
                if local:
                    copy.wait()
                else:
                    copy.wait_recv()

    def entry_sent(u):
        @pl.when(jnp.logical_not(stays(u)))
        def _():
            first_hop(u, False, False).wait_send()

        @pl.when(token_block(u) != i)
        def _():
            second_hop(u, i).wait_send()

    def a_copy(slot, u, index, device):
        window = abuf.at[slot, rows_of(u)]
        return pltpu.make_async_remote_copy(
            src_ref=window,
            dst_ref=window,
            send_sem=a_send.at[index],
            recv_sem=a_recv.at[slot, u],
            device_id=device,
            device_id_type=MESH,
        )

    def b_copy(slot, u, index, device):
        window = bbuf.at[slot] if u is None else bbuf.at[slot, rows_of(u)]
        return pltpu.make_async_remote_copy(
            src_ref=window,
            dst_ref=window,
            send_sem=b_send.at[index],
            recv_sem=b_recv.at[slot, u or 0],
            device_id=device,
            device_id_type=MESH,
        )

    pending = {a_copy: [], b_copy: []}

    def send(make, slot, u, device):
        copy = make(slot, u, len(pending[make]), device)
        pending[make].append(copy)
        copy.start()

    def arrive(make, slot, u):
        make(slot, u, 0, place(dx=1)).wait_recv()

    def z_slot(distance):
        return ((z + distance + NZ) % NZ) * 2 + c

    def ring_own(u):
        for step in (1, -1):
            send(b_copy, i, u, place(dz=step))

    def ring(distance, u, step):
        slot = z_slot(-step * distance)
        arrive(b_copy, slot, u)
        if distance < 3 or passes_on(u, step):
            send(b_copy, slot, u, place(dz=step))
        rung[distance, step] = rung.get((distance, step), 0) + 1
        if rung[distance, step] == UNITS:
            send(b_copy, slot, None, place(other=True))

    rung = {}

    def ring_last(u):
        arrive(b_copy, z_slot(4), u)

    def a_slot(u, p, s):
        dx, dy = (p, s) if u < 2 else (s, p)
        where = ((y + dy + NY) % NY) * NX + (x + dx + NX) % NX
        return (where - i - SHIFT[u] + 2 * PARTS) % PARTS

    def primary(u, step):
        return place(dx=step) if u < 2 else place(dy=step)

    def secondary(u, step):
        return place(dy=step) if u < 2 else place(dx=step)

    def passes_on(u, step):
        return u % 2 == (0 if step == 1 else 1)

    def first_step(u):
        entered(u)
        for step in (1, -1):
            send(a_copy, a_slot(u, 0, 0), u, primary(u, step))
        for step in (1, -1):
            send(a_copy, a_slot(u, 0, 0), u, secondary(u, step))

    def primary_near(u, step):
        slot = a_slot(u, -step, 0)
        arrive(a_copy, slot, u)
        if passes_on(u, step):
            send(a_copy, slot, u, primary(u, step))
        for side in (1, -1):
            send(a_copy, slot, u, secondary(u, side))

    def primary_far(u):
        slot = a_slot(u, 2, 0)
        arrive(a_copy, slot, u)
        for side in (1, -1):
            send(a_copy, slot, u, secondary(u, side))

    def secondary_near(u, p, step):
        slot = a_slot(u, p, -step)
        arrive(a_copy, slot, u)
        if passes_on(u, step):
            send(a_copy, slot, u, secondary(u, step))

    def columns_of(p, s):
        slots = [a_slot(u, p, s) for u in range(UNITS)]
        return [
            jnp.concatenate([buf[slot, rows_of(u)] for u, slot in enumerate(slots)], axis=0)
            for buf in (abuf, bbuf)
        ]

    def multiply(places):
        first, second = (
            jnp.concatenate(parts, axis=0) for parts in zip(*(columns_of(p, s) for p, s in places))
        )
        return lax.dot_general(
            first, second, (((0,), (0,)), ((), ())), preferred_element_type=jnp.float32
        )

    actions = {
        "enter": start_first_hop, "own": ring_own, "forward": forward, "first": first_step,
        "near": primary_near, "far": primary_far, "side": secondary_near, "ring": ring,
        "last": ring_last,
    }
    loaded = False
    for name, *where in ORDER:
        if name == "own" and not loaded:
            load.wait()
            send(b_copy, i, None, place(other=True))
            loaded = True
        actions[name](*where)
    send(b_copy, z_slot(4), None, place(other=True))
    for distance in range(NZ):
        arrive(b_copy, ((z + distance) % NZ) * 2 + 1 - c, None)
    g_ref[...] = multiply([(p, s) for s in (0, -1, 1) for p in (0, -1, 1, 2)])
    for p in (0, -1, 1, 2):
        for u in range(UNITS):
            arrive(a_copy, a_slot(u, p, 2), u)
    g_ref[...] = scale * (g_ref[...] + multiply([(p, 2) for p in (0, -1, 1, 2)]))

    for copies in pending.values():
        for copy in copies:
            copy.wait_send()
    for u in range(UNITS):
        entry_sent(u)


def gather_product(inputs, out_grads, scale):
    rows, width = inputs.shape
    columns = out_grads.shape[1]
    return pl.pallas_call(
        lambda *refs: gather_kernel(scale, *refs),
        out_shape=jax.ShapeDtypeStruct((width, columns), jnp.float32),
        in_specs=[pl.BlockSpec(memory_space=pltpu.HBM)] * 2,
        out_specs=pl.BlockSpec(memory_space=pltpu.VMEM),
        scratch_shapes=[
            pltpu.VMEM((PARTS, rows, width), jnp.bfloat16),
            pltpu.VMEM((PARTS, rows, columns), jnp.bfloat16),
            pltpu.VMEM((UNITS, rows // UNITS, width), jnp.bfloat16),
            pltpu.SemaphoreType.DMA((1,)),
            pltpu.SemaphoreType.DMA((UNITS,)),
            pltpu.SemaphoreType.DMA((UNITS,)),
            pltpu.SemaphoreType.DMA((UNITS,)),
            pltpu.SemaphoreType.DMA((UNITS,)),
            pltpu.SemaphoreType.DMA((60,)),
            pltpu.SemaphoreType.DMA((PARTS, UNITS)),
            pltpu.SemaphoreType.DMA((40,)),
            pltpu.SemaphoreType.DMA((PARTS, UNITS)),
        ],
        compiler_params=pltpu.CompilerParams(
            collective_id=0, has_side_effects=True, vmem_limit_bytes=24 * 1024 * 1024
        ),
        cost_estimate=pl.CostEstimate(
            flops=30_000_000_000, bytes_accessed=1 << 20, transcendentals=0
        ),
        name="gather_product",
    )(*(pltpu.with_memory_space_constraint(a, pltpu.HBM) for a in (inputs, out_grads)))


def split(value):
    high = value.astype(jnp.bfloat16)
    return high, (value - high.astype(jnp.float32)).astype(jnp.bfloat16)


def dot(first, second):
    return jnp.dot(first, second, preferred_element_type=jnp.float32)


SLOTS = 21
G, GT, T = 18, 19, 20
M0, F1, S, Q, M1, F2, X2, F3, X3 = range(9)
TILE = 256


def roots_kernel(
    ages, g_ref, left_old, right_old, left_roots, right_roots,
    precond, left_new, right_new, new, final, high, low, store_sem,
):
    order = g_ref.shape[0]
    due = ages[lax.axis_index("dp"), lax.axis_index("mp")] >= PERIOD
    tiles = range(order // TILE)
    spans = [pl.ds(tile * TILE, TILE) for tile in tiles]
    everything = pl.ds(0, order)
    blocks = [(0, 0), (0, 1), (1, 1)]
    diagonal = lax.broadcasted_iota(jnp.int32, (TILE, TILE), 0) == lax.broadcasted_iota(
        jnp.int32, (TILE, TILE), 1
    )

    def put(slot, rows, columns, value):
        high[slot, rows, columns], low[slot, rows, columns] = split(value)

    def multiply(first, second, rows, columns):
        right_high = high[second, :, columns]
        left_high = high[first, rows, :]
        return (
            dot(left_high, right_high)
            + dot(left_high, low[second, :, columns])
            + dot(low[first, rows, :], right_high)
        )

    def symmetric(first, second, use):
        for m, n in blocks:
            value = multiply(first, second, spans[m], spans[n])
            use(m, n, value)
            if m != n:
                use(n, m, value.T)

    def on_diagonal(m, n, value, shift):
        return jnp.where(diagonal, value + shift, value) if m == n else value

    for tile in tiles:
        part = g_ref[:, spans[tile]]
        put(G, everything, spans[tile], part)
        put(GT, spans[tile], everything, part.T)

    stores = []
    totals = []
    for side, (first, second, old, out) in enumerate(
        ((G, GT, left_old, left_new), (GT, G, right_old, right_new))
    ):
        squares = []

        def use(m, n, value):
            stat = decay_rate * old[spans[m], spans[n]] + value * (1.0 / order)
            new[side, spans[m], spans[n]] = stat
            ridged = on_diagonal(m, n, stat, ridge)
            squares.append(jnp.sum(ridged * ridged))

        symmetric(first, second, use)
        totals.append(sum(squares))
        store = pltpu.make_async_copy(new.at[side], out, store_sem.at[side])
        store.start()
        stores.append(store)

    def put_factor(slot, m, n, moment):
        put(slot, spans[m], spans[n], on_diagonal(m, n, -0.25 * moment, 1.25))

    @pl.when(due)
    def _():
        scales = []
        for side in range(2):
            base = 9 * side
            scale = jnp.sqrt(jnp.full((1, TILE), totals[side]) / order + 1e-06)
            inverse = 1.0 / scale
            scales.append(jnp.exp(-0.25 * jnp.log(scale)))
            for m in tiles:
                for n in tiles:
                    moment = on_diagonal(m, n, new[side, spans[m], spans[n]], ridge) * inverse
                    put(base + M0, spans[m], spans[n], moment)
                    put_factor(base + F1, m, n, moment)

        def both(first, second, use):
            for side in range(2):
                base = 9 * side
                symmetric(base + first, base + second, lambda m, n, v: use(side, base, m, n, v))

        def into(slot):
            return lambda side, base, m, n, v: put(base + slot, spans[m], spans[n], v)

        def moment_and_factor(side, base, m, n, value):
            put(base + M1, spans[m], spans[n], value)
            put_factor(base + F2, m, n, value)

        both(F1, F1, into(S))
        both(S, S, into(Q))
        both(Q, M0, moment_and_factor)
        both(F2, F2, into(S))
        both(
            F1, F2,
            lambda side, base, m, n, v: put(base + X2, spans[m], spans[n], v * scales[side]),
        )
        both(S, S, into(Q))
        both(Q, M1, lambda side, base, m, n, v: put_factor(base + F3, m, n, v))
        both(X2, F3, into(X3))

    @pl.when(jnp.logical_not(due))
    def _():
        for side, root in enumerate((left_roots, right_roots)):
            for span in spans:
                put(9 * side + X3, everything, span, root[:, span])

    for span in spans:
        put(T, everything, span, multiply(X3, G, everything, span))
    for tile, span in enumerate(spans):
        final[:, span] = multiply(T, 9 + X3, everything, span)
        store = pltpu.make_async_copy(
            final.at[:, span], precond.at[:, span], store_sem.at[2 + tile]
        )
        store.start()
        stores.append(store)
    for store in stores:
        store.wait()


def shards(inputs, out_grads, left_old, right_old, left_roots, right_roots, ages):
    order = left_old.shape[0]
    tokens_all = out_grads.shape[0] * lax.axis_size("dp")
    gradient = gather_product(inputs, out_grads, tokens_all ** (-0.5))
    outside = pl.BlockSpec(memory_space=pltpu.HBM)
    inside = pl.BlockSpec(memory_space=pltpu.VMEM)
    whole = jax.ShapeDtypeStruct((order, order), jnp.float32)
    return pl.pallas_call(
        roots_kernel,
        out_shape=(whole, whole, whole),
        in_specs=[
            pl.BlockSpec(memory_space=pltpu.SMEM),
            inside, inside, inside, inside, inside,
        ],
        out_specs=(outside, outside, outside),
        scratch_shapes=[
            pltpu.VMEM((2, order, order), jnp.float32),
            pltpu.VMEM((order, order), jnp.float32),
            pltpu.VMEM((SLOTS, order, order), jnp.bfloat16),
            pltpu.VMEM((SLOTS, order, order), jnp.bfloat16),
            pltpu.SemaphoreType.DMA((4,)),
        ],
        compiler_params=pltpu.CompilerParams(vmem_limit_bytes=40 * 1024 * 1024),
        name="roots",
    )(ages, gradient, left_old, right_old, left_roots, right_roots)


def solution(mesh):
    in_specs = (
        P("dp", "mp"),
        P("dp", "mp"),
        P("dp", "mp"),
        P("dp", "mp"),
        P("dp", "mp"),
        P("dp", "mp"),
        P(),
    )
    out_specs = (P("dp", "mp"), P("dp", "mp"), P("dp", "mp"))
    return jax.shard_map(shards, mesh=mesh, in_specs=in_specs, out_specs=out_specs, check_vma=False)
```

profile of v0, /device:TPU:1, one launch (start us, length us, event | category | flops | bytes accessed | tf_op | source)
XLA Modules:
  0.0 72.4 jit_solution(3408307617502549761)
XLA Ops:
  0.6 0.0 copy-start.4
  0.6 0.0 copy-start.3
  0.7 0.0 copy-start.2
  0.7 0.0 copy-start.1
  0.7 0.0 copy-start
  0.7 55.6 %gather_product.1.g_ref = f32[512,512]{1,0:T(8,128)S(1)} custom-call(bf16[256,512]{1,0:T(8,128)(2,1)} %refs_0_.1, bf16[256,512]{1,0:T(8,128)(2,1)} %refs_1_.1), custom_call_target="tpu_custom_call" | custom-call | flops 30000001024 | bytes 1048576 | tf_op jit(solution)/shard_map/gather_product/pallas_call | solution.py:301
  56.3 0.0 copy-done.4
  56.3 0.0 copy-done.3
  56.3 0.0 copy-done.2
  56.3 0.0 copy-done.1
  56.3 0.0 copy-done
  56.3 15.9 %roots.1 = (f32[512,512]{1,0:T(8,128)}, f32[512,512]{1,0:T(8,128)}, f32[512,512]{1,0:T(8,128)}) custom-call(s32[16,16]{1,0:T(8,128)S(1)} %copy-done.4, f32[512,512]{1,0:T(8,128)S(1)} %gather_product.1.g_ref, f32[512,512]{1,0:T(8,128)S(1)} %copy-done, f32[512,512]{1,0:T(8,128)S(1)} %copy-done.1, f32[512,512]{1,0:T(8,128)S(1)} %copy-done.2, ...), custom_call_target="tpu_custom_call" | custom-call | tf_op jit(solution)/shard_map/roots/pallas_call | solution.py:472
Async XLA Ops:
  0.6 55.7 %copy-start.4 = (s32[16,16]{1,0:T(8,128)S(1)}, s32[16,16]{1,0:T(8,128)}, u32[]{:S(2)}) copy-start(s32[16,16]{1,0:T(8,128)} %ages.1) | copy-start | bytes 3076
  0.6 55.7 %copy-start.3 = (f32[512,512]{1,0:T(8,128)S(1)}, f32[512,512]{1,0:T(8,128)}, u32[]{:S(2)}) copy-start(f32[512,512]{1,0:T(8,128)} %right_roots.1) | copy-start | bytes 3145732
  0.7 55.7 %copy-start.2 = (f32[512,512]{1,0:T(8,128)S(1)}, f32[512,512]{1,0:T(8,128)}, u32[]{:S(2)}) copy-start(f32[512,512]{1,0:T(8,128)} %left_roots.1) | copy-start | bytes 3145732
  0.7 55.7 %copy-start.1 = (f32[512,512]{1,0:T(8,128)S(1)}, f32[512,512]{1,0:T(8,128)}, u32[]{:S(2)}) copy-start(f32[512,512]{1,0:T(8,128)} %right_old.1) | copy-start | bytes 3145732
  0.7 55.7 %copy-start = (f32[512,512]{1,0:T(8,128)S(1)}, f32[512,512]{1,0:T(8,128)}, u32[]{:S(2)}) copy-start(f32[512,512]{1,0:T(8,128)} %left_old.1) | copy-start | bytes 3145732
where the time goes:
time: 72.5 us; the launch traced here: 72.4 us
  Pallas kernels  71.5 us (99%)
  between operations  0.88 us (1%)
    pallas_call x1, Pallas kernels, gather_product(): pl.pallas_call(lambda *refs: gather_kernel(scale, *refs), out_shape=jax.S...  55.6 us
    pallas_call x1, Pallas kernels, shards(): pl.pallas_call(roots_kernel, out_shape=(whole, whole, whole), in_specs=[p...  15.9 us

commit v1 on v0

--- a/solution.py
+++ b/solution.py
@@ -18,28 +18,30 @@
 UNITS = 4
 SHIFT = (0, 6, 8, 14)
 ORDER = (
-    ("enter", 0), ("enter", 1), ("enter", 2), ("enter", 3), ("own", 0), ("own", 1), ("forward", 0),
-    ("forward", 1), ("forward", 2), ("forward", 3), ("ring", 1, 0, -1), ("first", 0), ("first", 1),
-    ("first", 2), ("first", 3), ("side", 0, 0, 1), ("ring", 1, 0, 1), ("near", 0, 1), ("near", 0, -1),
-    ("own", 2), ("own", 3), ("near", 1, -1), ("near", 3, -1), ("ring", 1, 2, 1), ("side", 0, 0, -1),
-    ("side", 2, 0, -1), ("ring", 1, 3, -1), ("ring", 1, 1, -1), ("side", 1, 0, -1), ("ring", 1, 3, 1),
-    ("near", 2, 1), ("near", 2, -1), ("ring", 1, 1, 1), ("near", 1, 1), ("near", 3, 1),
-    ("side", 2, 0, 1), ("side", 3, 0, -1), ("ring", 1, 2, -1), ("ring", 2, 0, 1), ("ring", 2, 0, -1),
-    ("far", 0), ("side", 2, -1, -1), ("side", 1, 0, 1), ("ring", 2, 1, 1), ("far", 3), ("far", 2),
-    ("ring", 2, 2, 1), ("far", 1), ("side", 0, -1, 1), ("ring", 2, 3, 1), ("ring", 2, 1, -1),
-    ("side", 3, -1, 1), ("ring", 2, 3, -1), ("side", 0, 1, -1), ("side", 3, 1, 1), ("side", 3, 0, 1),
-    ("side", 3, 1, -1), ("side", 0, 2, -1), ("ring", 2, 2, -1), ("side", 1, -1, -1), ("side", 1, 1, 1),
-    ("side", 1, -1, 1), ("side", 3, -1, -1), ("side", 0, -1, -1), ("side", 0, 1, 1), ("ring", 3, 1, 1),
-    ("ring", 3, 0, 1), ("side", 2, 1, 1), ("side", 1, 2, 1), ("side", 1, 1, -1), ("side", 2, -1, 1),
-    ("ring", 3, 1, -1), ("side", 2, 2, -1), ("side", 0, 2, 1), ("side", 1, 2, -1), ("side", 2, 1, -1),
-    ("ring", 3, 3, -1), ("ring", 3, 2, -1), ("side", 2, 2, 1), ("ring", 3, 3, 1), ("side", 3, 2, 1),
-    ("ring", 3, 0, -1), ("side", 3, 2, -1), ("ring", 3, 2, 1), ("last", 1), ("last", 2), ("last", 3),
-    ("last", 0),
+    ("enter", 0), ("enter", 1), ("enter", 2), ("enter", 3), ("own", 0), ("cross", 0, 1), ("own", 1),
+    ("own", 2), ("own", 3), ("forward", 0), ("forward", 1), ("ring", 1, 0, 1), ("ring", 1, 0, -1),
+    ("forward", 2), ("forward", 3), ("ring", 1, 1, 1), ("ring", 1, 1, -1), ("first", 0),
+    ("ring", 1, 2, 1), ("ring", 1, 2, -1), ("first", 1), ("ring", 1, 3, 1), ("cross", 1, 1),
+    ("ring", 1, 3, -1), ("cross", 1, -1), ("first", 2), ("ring", 2, 0, 1), ("ring", 2, 0, -1),
+    ("first", 3), ("near", 0, 1), ("near", 0, -1), ("side", 0, 0, 1), ("side", 0, 0, -1),
+    ("near", 1, 1), ("near", 1, -1), ("ring", 2, 1, 1), ("ring", 2, 1, -1), ("side", 1, 0, 1),
+    ("side", 1, 0, -1), ("near", 2, 1), ("near", 2, -1), ("ring", 2, 2, 1), ("ring", 2, 2, -1),
+    ("side", 2, 0, 1), ("side", 2, 0, -1), ("near", 3, 1), ("near", 3, -1), ("side", 3, 0, 1),
+    ("side", 3, 0, -1), ("ring", 2, 3, 1), ("cross", 2, 1), ("ring", 2, 3, -1), ("cross", 2, -1),
+    ("far", 0), ("far", 1), ("ring", 3, 0, 1), ("ring", 3, 0, -1), ("far", 2), ("far", 3),
+    ("side", 0, -1, 1), ("side", 0, -1, -1), ("ring", 3, 1, 1), ("ring", 3, 1, -1), ("side", 1, -1, 1),
+    ("side", 1, -1, -1), ("side", 2, -1, 1), ("side", 2, -1, -1), ("ring", 3, 2, 1),
+    ("ring", 3, 2, -1), ("side", 3, -1, 1), ("side", 3, -1, -1), ("side", 0, 1, 1), ("side", 0, 1, -1),
+    ("side", 1, 1, 1), ("side", 1, 1, -1), ("ring", 3, 3, 1), ("cross", 3, 1), ("ring", 3, 3, -1),
+    ("cross", 3, -1), ("side", 2, 1, 1), ("side", 2, 1, -1), ("side", 3, 1, 1), ("side", 3, 1, -1),
+    ("side", 0, 2, 1), ("side", 0, 2, -1), ("side", 1, 2, 1), ("side", 1, 2, -1), ("side", 2, 2, 1),
+    ("side", 2, 2, -1), ("side", 3, 2, 1), ("side", 3, 2, -1), ("last", 0), ("last", 1), ("last", 2),
+    ("last", 3), ("cross", 4, 1),
 )
 
 
 def gather_kernel(
-    scale, a_hbm, b_hbm, g_ref, abuf, bbuf, stage, load_sem, s_send, s_recv, t_send, t_recv,
+    scale, a_hbm, b_hbm, g_ref, abuf, bbuf, own, stage, load_sem, s_send, s_recv, t_send, t_recv,
     a_send, a_recv, b_send, b_recv,
 ):
     rows, width = a_hbm.shape
@@ -74,6 +76,8 @@
     def rows_of(u):
         return pl.ds(u * count, count)
 
+    own_load = pltpu.make_async_copy(a_hbm, own, load_sem.at[1])
+    own_load.start()
     load = pltpu.make_async_copy(b_hbm, bbuf.at[i], load_sem.at[0])
     load.start()
     barrier = pltpu.get_barrier_semaphore()
@@ -85,9 +89,10 @@
     for device in greeted:
         pl.semaphore_signal(barrier, inc=1, device_id=device, device_id_type=MESH)
     pl.semaphore_wait(barrier, len(greeted))
+    own_load.wait()
 
     def first_hop(u, final, local):
-        source = a_hbm.at[rows_of(u)]
+        source = (a_hbm if local else own).at[rows_of(u)]
         goal = abuf.at[i, rows_of(u)] if final else stage.at[u]
         arrived = (t_recv if final else s_recv).at[u]
         if local:
@@ -202,11 +207,9 @@
         arrive(b_copy, slot, u)
         if distance < 3 or passes_on(u, step):
             send(b_copy, slot, u, place(dz=step))
-        rung[distance, step] = rung.get((distance, step), 0) + 1
-        if rung[distance, step] == UNITS:
-            send(b_copy, slot, None, place(other=True))
-
-    rung = {}
+
+    def cross(distance, step):
+        send(b_copy, z_slot(-step * distance), None, place(other=True))
 
     def ring_last(u):
         arrive(b_copy, z_slot(4), u)
@@ -270,16 +273,14 @@
     actions = {
         "enter": start_first_hop, "own": ring_own, "forward": forward, "first": first_step,
         "near": primary_near, "far": primary_far, "side": secondary_near, "ring": ring,
-        "last": ring_last,
+        "last": ring_last, "cross": cross,
     }
     loaded = False
     for name, *where in ORDER:
         if name == "own" and not loaded:
             load.wait()
-            send(b_copy, i, None, place(other=True))
             loaded = True
         actions[name](*where)
-    send(b_copy, z_slot(4), None, place(other=True))
     for distance in range(NZ):
         arrive(b_copy, ((z + distance) % NZ) * 2 + 1 - c, None)
     g_ref[...] = multiply([(p, s) for s in (0, -1, 1) for p in (0, -1, 1, 2)])
@@ -306,8 +307,9 @@
         scratch_shapes=[
             pltpu.VMEM((PARTS, rows, width), jnp.bfloat16),
             pltpu.VMEM((PARTS, rows, columns), jnp.bfloat16),
+            pltpu.VMEM((rows, width), jnp.bfloat16),
             pltpu.VMEM((UNITS, rows // UNITS, width), jnp.bfloat16),
-            pltpu.SemaphoreType.DMA((1,)),
+            pltpu.SemaphoreType.DMA((2,)),
             pltpu.SemaphoreType.DMA((UNITS,)),
             pltpu.SemaphoreType.DMA((UNITS,)),
             pltpu.SemaphoreType.DMA((UNITS,)),

time: 72.5 us -> 67.8 us (0.935)
  the two profiles are of different devices: /device:TPU:1 before, /device:TPU:33 now
where the time goes in v1:
time: 67.8 us; the launch traced here: 66.9 us
  Pallas kernels  66 us (97%)
  between operations  0.88 us (1%)
    pallas_call x1, Pallas kernels, gather_product(): pl.pallas_call(lambda *refs: gather_kernel(scale, *refs), out_shape=jax.S...  50.1 us
    pallas_call x1, Pallas kernels, shards(): pl.pallas_call(roots_kernel, out_shape=(whole, whole, whole), in_specs=[p...  15.9 us

profile of v1, /device:TPU:33, one launch (start us, length us, event | category | flops | bytes accessed | tf_op | source)
XLA Modules:
  0.0 66.9 jit_solution(17956121042452946796)
XLA Ops:
  0.6 0.0 copy-start.4
  0.6 0.0 copy-start.3
  0.7 0.0 copy-start.2
  0.7 0.0 copy-start.1
  0.7 0.0 copy-start
  0.7 50.1 %gather_product.1.g_ref = f32[512,512]{1,0:T(8,128)S(1)} custom-call(bf16[256,512]{1,0:T(8,128)(2,1)} %refs_0_.1, bf16[256,512]{1,0:T(8,128)(2,1)} %refs_1_.1), custom_call_target="tpu_custom_call" | custom-call | flops 30000001024 | bytes 1048576 | tf_op jit(solution)/shard_map/gather_product/pallas_call | solution.py:302
  50.8 0.0 copy-done.4
  50.8 0.0 copy-done.3
  50.8 0.0 copy-done.2
  50.8 0.0 copy-done.1
  50.9 0.0 copy-done
  50.9 15.9 %roots.1 = (f32[512,512]{1,0:T(8,128)}, f32[512,512]{1,0:T(8,128)}, f32[512,512]{1,0:T(8,128)}) custom-call(s32[16,16]{1,0:T(8,128)S(1)} %copy-done.4, f32[512,512]{1,0:T(8,128)S(1)} %gather_product.1.g_ref, f32[512,512]{1,0:T(8,128)S(1)} %copy-done, f32[512,512]{1,0:T(8,128)S(1)} %copy-done.1, f32[512,512]{1,0:T(8,128)S(1)} %copy-done.2, ...), custom_call_target="tpu_custom_call" | custom-call | tf_op jit(solution)/shard_map/roots/pallas_call | solution.py:474
Async XLA Ops:
  0.6 50.2 %copy-start.4 = (s32[16,16]{1,0:T(8,128)S(1)}, s32[16,16]{1,0:T(8,128)}, u32[]{:S(2)}) copy-start(s32[16,16]{1,0:T(8,128)} %ages.1) | copy-start | bytes 3076
  0.6 50.2 %copy-start.3 = (f32[512,512]{1,0:T(8,128)S(1)}, f32[512,512]{1,0:T(8,128)}, u32[]{:S(2)}) copy-start(f32[512,512]{1,0:T(8,128)} %right_roots.1) | copy-start | bytes 3145732
  0.7 50.2 %copy-start.2 = (f32[512,512]{1,0:T(8,128)S(1)}, f32[512,512]{1,0:T(8,128)}, u32[]{:S(2)}) copy-start(f32[512,512]{1,0:T(8,128)} %left_roots.1) | copy-start | bytes 3145732
  0.7 50.2 %copy-start.1 = (f32[512,512]{1,0:T(8,128)S(1)}, f32[512,512]{1,0:T(8,128)}, u32[]{:S(2)}) copy-start(f32[512,512]{1,0:T(8,128)} %right_old.1) | copy-start | bytes 3145732
  0.7 50.2 %copy-start = (f32[512,512]{1,0:T(8,128)S(1)}, f32[512,512]{1,0:T(8,128)}, u32[]{:S(2)}) copy-start(f32[512,512]{1,0:T(8,128)} %left_old.1) | copy-start | bytes 3145732

commit v2 on v1

--- a/solution.py
+++ b/solution.py
@@ -346,7 +346,7 @@
 
 def roots_kernel(
     ages, g_ref, left_old, right_old, left_roots, right_roots,
-    precond, left_new, right_new, new, final, high, low, store_sem,
+    precond, left_new, right_new, new, final, cross, high, low, store_sem,
 ):
     order = g_ref.shape[0]
     due = ages[lax.axis_index("dp"), lax.axis_index("mp")] >= PERIOD
@@ -377,6 +377,20 @@
             if m != n:
                 use(n, m, value.T)
 
+    def square(first, second, use, side):
+        for m in tiles:
+            for n in tiles:
+                cross[side, spans[m], spans[n]] = dot(
+                    high[first, spans[m], :], low[second, :, spans[n]]
+                )
+        for m, n in blocks:
+            value = dot(high[first, spans[m], :], high[second, :, spans[n]])
+            other = cross[side, spans[n], spans[m]]
+            value = value + (cross[side, spans[m], spans[n]] + other.T)
+            use(m, n, value)
+            if m != n:
+                use(n, m, value.T)
+
     def on_diagonal(m, n, value, shift):
         return jnp.where(diagonal, value + shift, value) if m == n else value
 
@@ -398,7 +412,7 @@
             ridged = on_diagonal(m, n, stat, ridge)
             squares.append(jnp.sum(ridged * ridged))
 
-        symmetric(first, second, use)
+        square(first, second, use, side)
         totals.append(sum(squares))
         store = pltpu.make_async_copy(new.at[side], out, store_sem.at[side])
         store.start()
@@ -424,7 +438,14 @@
         def both(first, second, use):
             for side in range(2):
                 base = 9 * side
-                symmetric(base + first, base + second, lambda m, n, v: use(side, base, m, n, v))
+
+                def here(m, n, value):
+                    use(side, base, m, n, value)
+
+                if first == second:
+                    square(base + first, base + second, here, side)
+                else:
+                    symmetric(base + first, base + second, here)
 
         def into(slot):
             return lambda side, base, m, n, v: put(base + slot, spans[m], spans[n], v)
@@ -482,6 +503,7 @@
         scratch_shapes=[
             pltpu.VMEM((2, order, order), jnp.float32),
             pltpu.VMEM((order, order), jnp.float32),
+            pltpu.VMEM((2, order, order), jnp.float32),
             pltpu.VMEM((SLOTS, order, order), jnp.bfloat16),
             pltpu.VMEM((SLOTS, order, order), jnp.bfloat16),
             pltpu.SemaphoreType.DMA((4,)),

time: 67.8 us -> 67.5 us (level)
  the two profiles are of different devices: /device:TPU:33 before, /device:TPU:3 now
where the time goes in v2:
time: 67.5 us; the launch traced here: 67.3 us
  Pallas kernels  66.4 us (98%)
  between operations  0.88 us (1%)
    pallas_call x1, Pallas kernels, gather_product(): pl.pallas_call(lambda *refs: gather_kernel(scale, *refs), out_shape=jax.S...  51.5 us
    pallas_call x1, Pallas kernels, shards(): pl.pallas_call(roots_kernel, out_shape=(whole, whole, whole), in_specs=[p...  14.9 us

profile of v2, /device:TPU:3, one launch (start us, length us, event | category | flops | bytes accessed | tf_op | source)
XLA Modules:
  0.0 67.3 jit_solution(8283364779205658566)
XLA Ops:
  0.6 0.0 copy-start.4
  0.6 0.0 copy-start.3
  0.7 0.0 copy-start.2
  0.7 0.0 copy-start.1
  0.7 0.0 copy-start
  0.7 51.5 %gather_product.1.g_ref = f32[512,512]{1,0:T(8,128)S(1)} custom-call(bf16[256,512]{1,0:T(8,128)(2,1)} %refs_0_.1, bf16[256,512]{1,0:T(8,128)(2,1)} %refs_1_.1), custom_call_target="tpu_custom_call" | custom-call | flops 30000001024 | bytes 1048576 | tf_op jit(solution)/shard_map/gather_product/pallas_call | solution.py:302
  52.2 0.0 copy-done.4
  52.2 0.0 copy-done.3
  52.2 0.0 copy-done.2
  52.3 0.0 copy-done.1
  52.3 0.0 copy-done
  52.3 14.9 %roots.1 = (f32[512,512]{1,0:T(8,128)}, f32[512,512]{1,0:T(8,128)}, f32[512,512]{1,0:T(8,128)}) custom-call(s32[16,16]{1,0:T(8,128)S(1)} %copy-done.4, f32[512,512]{1,0:T(8,128)S(1)} %gather_product.1.g_ref, f32[512,512]{1,0:T(8,128)S(1)} %copy-done, f32[512,512]{1,0:T(8,128)S(1)} %copy-done.1, f32[512,512]{1,0:T(8,128)S(1)} %copy-done.2, ...), custom_call_target="tpu_custom_call" | custom-call | tf_op jit(solution)/shard_map/roots/pallas_call | solution.py:495
Async XLA Ops:
  0.6 51.6 %copy-start.4 = (s32[16,16]{1,0:T(8,128)S(1)}, s32[16,16]{1,0:T(8,128)}, u32[]{:S(2)}) copy-start(s32[16,16]{1,0:T(8,128)} %ages.1) | copy-start | bytes 3076
  0.6 51.6 %copy-start.3 = (f32[512,512]{1,0:T(8,128)S(1)}, f32[512,512]{1,0:T(8,128)}, u32[]{:S(2)}) copy-start(f32[512,512]{1,0:T(8,128)} %right_roots.1) | copy-start | bytes 3145732
  0.7 51.6 %copy-start.2 = (f32[512,512]{1,0:T(8,128)S(1)}, f32[512,512]{1,0:T(8,128)}, u32[]{:S(2)}) copy-start(f32[512,512]{1,0:T(8,128)} %left_roots.1) | copy-start | bytes 3145732
  0.7 51.6 %copy-start.1 = (f32[512,512]{1,0:T(8,128)S(1)}, f32[512,512]{1,0:T(8,128)}, u32[]{:S(2)}) copy-start(f32[512,512]{1,0:T(8,128)} %right_old.1) | copy-start | bytes 3145732
  0.7 51.6 %copy-start = (f32[512,512]{1,0:T(8,128)S(1)}, f32[512,512]{1,0:T(8,128)}, u32[]{:S(2)}) copy-start(f32[512,512]{1,0:T(8,128)} %left_old.1) | copy-start | bytes 3145732
